TPU v7x, 32 devices: a whole 2x2x4 slice. The times are simulated.
32 devices in a mesh: member: 2 (over y), lat: 16 (over z, x, core).
Axes of the slice: x: 2, y: 2, z: 4, core: 2. Of those that a mesh axis runs over, the one named last changes fastest.
Arguments:
- tracers: float32 [60, 4, 64, 1440], P('member', None, 'lat'), parts along dimension 0, may hold values from -6 to 6
- currents: float32 [4, 4, 64, 1440], P('member', None, 'lat'), parts along dimension 0, may hold values from -0.4 to 0.4
- column_levels: int32 [128, 1440], P(('member', 'lat')), parts along dimension 0, may hold values from 0 to 4
Outputs:
- advected: float32 [60, 4, 64, 1440], P('member', None, 'lat'), parts along dimension 0
There are 2 independent parts, one for each index of `member`. A program takes and returns all parts, laid end to end along the dimension named above; each array names one. Nothing has to cross between parts.
All inputs are finite; a program needn't handle non-finite values.
Results may differ from a plain program's by a relative error of at most 0.00002.
Values sent between devices are 32-bit elements; how exact they have to be, the bound alone decides.
A program may use at most 64 MiB of HBM per device.

v0:
```python
import functools

import jax
import jax.numpy as jnp
from jax import lax
from jax.experimental import pallas as pl
from jax.experimental.pallas import tpu as pltpu
from jax.sharding import PartitionSpec as P

LANES = 128
SUB = 8
WRAP = 4
HALO = 2
MESH = pl.DeviceIdType.MESH


def wrapped(x, nlon):
    rest = nlon % LANES
    whole = nlon - rest
    tail = jnp.concatenate([x[:, whole:], x[:, : LANES - rest]], axis=1)
    lane = lax.broadcasted_iota(jnp.int32, tail.shape, 1)
    tail = jnp.where(lane >= LANES - WRAP, pltpu.roll(tail, LANES - rest, 1), tail)
    return jnp.concatenate([x[:, :whole], tail], axis=1)


def joined(main, tail, rest):
    lane = lax.broadcasted_iota(jnp.int32, tail.shape, 1)
    west = pltpu.roll(tail, LANES - rest, 1)
    tail = jnp.where(lane < rest, tail, pltpu.roll(main[:, :LANES], rest, 1))
    tail = jnp.where(lane >= LANES - WRAP, west, tail)
    return jnp.concatenate([main, tail], axis=1)


def packed(a, b, rest):
    lane = lax.broadcasted_iota(jnp.int32, a.shape, 1)
    both = jnp.where(lane < rest, a, pltpu.roll(b, rest, 1))
    other = pltpu.roll(pltpu.roll(both, SUB // 2, 0), LANES // 2, 1)
    return jnp.where(lane < LANES // 2, both, other)[: SUB // 2]


def unpacked(half, rest):
    x = jnp.concatenate([half, half], axis=0)
    row = lax.broadcasted_iota(jnp.int32, x.shape, 0)
    x = jnp.where(row < SUB // 2, x, pltpu.roll(x, LANES // 2, 1))
    return x, pltpu.roll(x, LANES - rest, 1)


def face_terms(c, opened):
    c = c * opened * (1.0 / 12.0)
    m = jnp.abs(c)
    return -c - m, 7.0 * c + 3.0 * m, 7.0 * c - 3.0 * m, m - c


def mirrored(tiles, nlon):
    count = len(tiles)
    rest = nlon % LANES
    row = lax.broadcasted_iota(jnp.int32, (LANES, LANES), 0)
    col = lax.broadcasted_iota(jnp.int32, (LANES, LANES), 1)
    near = jnp.where((row + col == rest - 1), 1.0, 0.0).astype(jnp.float32)
    far = jnp.where((row + col == LANES + rest - 1), 1.0, 0.0).astype(jnp.float32)
    dot = functools.partial(
        jnp.dot, precision=lax.Precision.HIGHEST, preferred_element_type=jnp.float32
    )
    return [
        dot(tiles[(count - 1 - q) % count], near) + dot(tiles[(count - 2 - q) % count], far)
        for q in range(count)
    ]


def kernel(
    nlon, levels, group, raw_hbm, flow_hbm, lev_hbm, out_ref,
    raw, raw_flow, lev_ref, start, first, partial, lo, hi, relay, pack_up, pack_dn, pack_lo, pack_hi,
    flow, v_lo, v_hi, lev_up, lev_dn, lev_lo, lev_hi, coef, edge, wets, halo,
    load, aux_load, send_up, send_dn, recv_lo, recv_hi, relay_in, relay_out,
    psend_up, psend_dn, precv_lo, precv_hi, fsend, frecv,
):
    lat = lax.axis_size("lat")
    me = lax.axis_index("lat")
    rows, planes, width = start.shape
    rest = nlon % LANES
    whole = nlon - rest
    chunks = planes // SUB
    layers = lat // group
    layer = me // group
    place = me % group
    relays = layers > 1 and group > 2 and lat % group == 0
    has_lo = me > 0
    has_hi = me < lat - 1
    is_first = place == 0
    is_last = place == group - 1
    barrier = pltpu.get_barrier_semaphore()

    pairs = [(has_lo, -1), (has_hi, 1)]
    if relays:
        pairs += [
            (is_first, group - 1),
            (is_last, 1 - group),
            ((is_first | is_last) & (layer < layers - 1), group),
            ((is_first | is_last) & (layer > 0), -group),
        ]

    def part_of(g):
        return pl.ds(pl.multiple_of(g * SUB, SUB), SUB)

    def loading(g):
        part = part_of(g)
        return pltpu.make_async_copy(raw_hbm.at[part], raw.at[part], load.at[g])

    lev_load = pltpu.make_async_copy(lev_hbm, lev_ref, aux_load.at[0])
    flow_load = pltpu.make_async_copy(flow_hbm, raw_flow, aux_load.at[1])
    lev_load.start()
    loading(0).start()
    flow_load.start()

    for near, by in pairs:
        @pl.when(near)
        def _(by=by):
            pl.semaphore_signal(barrier, inc=1, device_id={"lat": me + by}, device_id_type=MESH)

    def load_rest(g, carry):
        loading(g).start()
        return carry

    lax.fori_loop(1, chunks, load_rest, 0)

    ranks = lax.rem(lax.broadcasted_iota(jnp.int32, (SUB, nlon), 0), levels)

    def wet_of(row):
        lev = jnp.broadcast_to(row, (SUB, nlon))
        return wrapped(jnp.where(ranks < lev, 1.0, 0.0), nlon)

    lev_load.wait()
    for k in range(rows):
        wets[k + 1] = wet_of(lev_ref[k : k + 1, :])
    lev_up[...] = lev_ref[rows - 1 : rows, :]
    lev_dn[...] = lev_ref[0:1, :]

    def put_packs(phase, g, tail):
        pack_up[phase, g] = packed(tail(rows - 2), tail(rows - 1), rest)
        pack_dn[phase, g] = packed(tail(0), tail(1), rest)

    def reorder(g):
        part = part_of(g)
        loading(g).wait()
        tails = []
        for k in range(rows):
            x = wrapped(raw[part, k, :], nlon) * wets[k + 1]
            start[k, part, :] = x
            tails.append(x[:, whole:])
        put_packs(0, g, lambda k: tails[k])

    reorder(0)
    flow_load.wait()
    for k in range(rows):
        for which in range(2):
            flow[which, k] = raw_flow[which, :, k, :]

    pl.semaphore_wait(barrier, sum(jnp.where(near, 1, 0) for near, _ in pairs))

    def remote(src, dst, s, r, by):
        return pltpu.make_async_remote_copy(
            src_ref=src, dst_ref=dst, send_sem=s, recv_sem=r,
            device_id={"lat": me + by}, device_id_type=MESH,
        )

    def flows(up):
        n = 0 if up else 2
        if up:
            pieces = [(flow.at[1, rows - 1], v_lo), (lev_up, lev_lo)]
        else:
            pieces = [(flow.at[1, 0], v_hi), (lev_dn, lev_hi)]
        by = 1 if up else -1
        return [
            remote(src, dst, fsend.at[n + i], frecv.at[n + i], by)
            for i, (src, dst) in enumerate(pieces)
        ]

    def main(phase, up, g, via):
        part = part_of(g)
        own = first if phase else start
        src = own.at[pl.ds(rows - HALO if up else 0, HALO), part, pl.ds(0, whole)]
        s = (send_up if up else send_dn).at[phase, g]
        if via:
            by = 1 - group if up else group - 1
            return remote(src, relay.at[phase, :, part], s, relay_in.at[phase, g], by)
        dst = (lo if up else hi).at[phase, :, part]
        r = (recv_lo if up else recv_hi).at[phase, g]
        return remote(src, dst, s, r, 1 if up else -1)

    def tails(phase, up, g):
        if up:
            return remote(pack_up.at[phase, g], pack_lo.at[phase, g],
                          psend_up.at[phase, g], precv_lo.at[phase, g], 1)
        return remote(pack_dn.at[phase, g], pack_hi.at[phase, g],
                      psend_dn.at[phase, g], precv_hi.at[phase, g], -1)

    def forward(phase, up, g):
        part = part_of(g)
        dst = (lo if up else hi).at[phase, :, part]
        r = (recv_lo if up else recv_hi).at[phase, g]
        return remote(relay.at[phase, :, part], dst, relay_out.at[phase, g], r,
                      group if up else -group)

    def detour(share, phase, g):
        left = chunks - 1 - g
        shift = 1 - phase
        return ((left + 1) * share + shift) // layers - (left * share + shift) // layers == 1

    def detour_up(phase, g):
        return detour(layers - 1 - layer, phase, g)

    def detour_dn(phase, g):
        return detour(layer, phase, g)

    def send(phase, g):
        for up, near, end, bent in (
            (True, has_hi, is_last, detour_up), (False, has_lo, is_first, detour_dn),
        ):
            if relays:
                by_relay = near & end & bent(phase, g)

                @pl.when(by_relay)
                def _(up=up):
                    main(phase, up, g, True).start()

                @pl.when(near & jnp.logical_not(by_relay))
                def _(up=up):
                    main(phase, up, g, False).start()
            else:
                @pl.when(near)
                def _(up=up):
                    main(phase, up, g, False).start()

            @pl.when(near)
            def _(up=up):
                tails(phase, up, g).start()

    def sent(phase, g):
        for up, near in ((True, has_hi), (False, has_lo)):
            @pl.when(near)
            def _(up=up):
                main(phase, up, g, False).wait_send()
                tails(phase, up, g).wait_send()

        if relays:
            for up, end, bent in ((True, is_first, detour_up), (False, is_last, detour_dn)):
                @pl.when(end & bent(phase, g))
                def _(up=up):
                    forward(phase, up, g).wait_send()

    def pass_on(phase, g):
        if relays:
            for up, end, bent in ((True, is_first, detour_up), (False, is_last, detour_dn)):
                @pl.when(end & bent(phase, g))
                def _(up=up):
                    main(phase, up, g, True).wait_recv()
                    forward(phase, up, g).start()

    def arrived(phase, g):
        for up, near in ((True, has_lo), (False, has_hi)):
            @pl.when(near)
            def _(up=up):
                main(phase, up, g, False).wait_recv()
                tails(phase, up, g).wait_recv()

    @pl.when(has_hi)
    def _():
        for c in flows(True):
            c.start()

    @pl.when(has_lo)
    def _():
        for c in flows(False):
            c.start()

    def begin(g, carry):
        @pl.when(g < chunks - 1)
        def _():
            reorder(g + 1)

        send(0, g)
        return carry

    lax.fori_loop(0, chunks, begin, 0)

    spans = [(q * LANES, min(LANES, nlon - q * LANES)) for q in range(width // LANES)]

    def tiles_of(x):
        lane = lax.broadcasted_iota(jnp.int32, (x.shape[0], LANES), 1)
        tiles = [x[:, q * LANES : (q + 1) * LANES] for q in range(width // LANES)]
        return tiles[:-1] + [jnp.where(lane < rest, tiles[-1], 0.0)]

    def fold(phase, g):
        part = part_of(g)
        own = first if phase else start
        x = jnp.concatenate([own[rows - 1 - k, part, :] for k in range(HALO)], axis=0)
        tiles = mirrored(tiles_of(x), nlon)
        for (at, n), t in zip(spans[:-1], tiles[:-1]):
            for k in range(HALO):
                hi[phase, k, part, at : at + n] = t[SUB * k : SUB * k + SUB]
        pack_hi[phase, g] = packed(tiles[-1][:SUB], tiles[-1][SUB:], rest)

    @pl.when(jnp.logical_not(has_lo))
    def _():
        v_lo[...] = jnp.zeros_like(v_lo)
        lev_lo[...] = jnp.zeros_like(lev_lo)
        lo[...] = jnp.zeros_like(lo)
        pack_lo[...] = jnp.zeros_like(pack_lo)

    @pl.when(jnp.logical_not(has_hi))
    def _():
        lev = jnp.broadcast_to(lev_ref[rows - 1 : rows, :].astype(jnp.float32), (SUB - levels, nlon))
        x = jnp.concatenate([flow[1, rows - 1], lev], axis=0)
        x = jnp.concatenate([x, jnp.zeros((SUB, width - nlon), jnp.float32)], axis=1)
        for (at, n), t in zip(spans, mirrored(tiles_of(x), nlon)):
            v_hi[:, at : at + n] = -t[:levels, :n]
            lev_hi[:, at : at + n] = (t[levels : levels + 1, :n] + 0.5).astype(jnp.int32)

        def fold_start(g, carry):
            fold(0, g)
            return carry

        lax.fori_loop(0, chunks, fold_start, 0)

    @pl.when(has_lo)
    def _():
        for c in flows(True):
            c.wait_recv()

    @pl.when(has_hi)
    def _():
        for c in flows(False):
            c.wait_recv()

    def shift(x, by):
        return pltpu.roll(x, (-by) % width, 1)

    wets[0] = wet_of(lev_lo[...])
    wets[rows + 1] = wet_of(lev_hi[...])

    def spread(x):
        return wrapped(jnp.concatenate([x] * (SUB // levels), axis=0), nlon)

    def v_row(j):
        if j < 0:
            return spread(v_lo[...])
        if j >= rows:
            return spread(v_hi[...])
        return spread(flow[1, j])

    def north_face(j):
        return face_terms(0.5 * (v_row(j) + v_row(j + 1)), wets[j + 1] * wets[j + 2])

    below = north_face(-1)
    for k in range(rows):
        wet = wets[k + 1]
        u = spread(flow[0, k])
        ea, eb, ed, ee = face_terms(0.5 * (u + shift(u, 1)), wet * shift(wet, 1))
        above = north_face(k)
        coef[k, 0] = wet * shift(ea, -1)
        coef[k, 1] = wet * (shift(eb, -1) - ea)
        coef[k, 2] = wet * (shift(ee, -1) - ed)
        coef[k, 3] = wet * -ee
        coef[k, 4] = wet * below[0]
        coef[k, 5] = wet * (below[1] - above[0])
        coef[k, 6] = wet * (below[3] - above[2])
        coef[k, 7] = wet * -above[3]
        coef[k, 8] = wet * (1.0 - eb + shift(ed, -1) - above[1] + below[2])
        below = above

    outer = [
        (k, 4 + i, k + d)
        for k in range(rows)
        for i, d in enumerate((-2, -1, 1, 2))
        if not 0 <= k + d < rows
    ]
    for n, (k, i, _) in enumerate(outer):
        edge[n] = 0.5 * coef[k, i]

    def section(get, k):
        f = get(k)
        total = coef[k, 8] * f
        total += coef[k, 0] * shift(f, -2)
        total += coef[k, 1] * shift(f, -1)
        total += coef[k, 2] * shift(f, 1)
        total += coef[k, 3] * shift(f, 2)
        for i, d in enumerate((-2, -1, 1, 2)):
            other = get(k + d)
            if other is not None:
                total += coef[k, 4 + i] * other
        return total

    def step(g, carry):
        pass_on(0, g)
        arrived(0, g)
        part = part_of(g)
        for low, mains, packs in ((0, lo, pack_lo), (HALO, hi, pack_hi)):
            for k, t in enumerate(unpacked(packs[0, g], rest)):
                halo[low + k] = joined(mains[0, k, part, :], t, rest)

        def field(j):
            if j < 0:
                return halo[j + HALO]
            if j >= rows:
                return halo[j - rows + HALO]
            return start[j, part, :]

        for k in range(rows):
            first[k, part, :] = section(field, k)
        put_packs(1, g, lambda k: first[k, part, whole:])

        def own(j):
            return first[j, part, :] if 0 <= j < rows else None

        for k in range(rows):
            partial[k, part, :] = 0.5 * (start[k, part, :] * wets[k + 1] + section(own, k))

        send(1, g)

        @pl.when(jnp.logical_not(has_hi))
        def _():
            fold(1, g)

        return carry

    lax.fori_loop(0, chunks, step, 0)

    def last(g, carry):
        pass_on(1, g)
        sent(0, g)
        arrived(1, g)
        part = part_of(g)
        others = {}
        for low, mains, packs in ((-HALO, lo, pack_lo), (rows, hi, pack_hi)):
            for k, t in enumerate(unpacked(packs[1, g], rest)):
                others[low + k] = jnp.concatenate([mains[1, k, part, :], t], axis=1)
        for k in range(rows):
            value = partial[k, part, :]
            for n, (at, _, j) in enumerate(outer):
                if at == k:
                    value += edge[n] * others[j]
            out_ref[part, k, :] = value[:, :nlon]
        return carry

    lax.fori_loop(0, chunks, last, 0)

    @pl.when(has_hi)
    def _():
        for c in flows(True):
            c.wait_send()

    @pl.when(has_lo)
    def _():
        for c in flows(False):
            c.wait_send()

    def finish(g, carry):
        sent(1, g)
        return carry

    lax.fori_loop(0, chunks, finish, 0)


def shards(group, tracers, currents, column_levels):
    count, levels, rows, nlon = tracers.shape
    planes = count * levels
    width = -(-(nlon + 2 * WRAP) // LANES) * LANES
    whole = nlon - nlon % LANES
    raw = tracers.reshape(planes, rows, nlon)
    chunks = planes // SUB
    hbm = pl.BlockSpec(memory_space=pltpu.HBM)
    vmem = pl.BlockSpec(memory_space=pltpu.VMEM)
    dma = pltpu.SemaphoreType.DMA

    def f32(*shape):
        return pltpu.VMEM(shape, jnp.float32)

    def i32(*shape):
        return pltpu.VMEM(shape, jnp.int32)

    pack = f32(2, chunks, SUB // 2, LANES)
    args = [pltpu.with_memory_space_constraint(x, pltpu.HBM) for x in (raw, currents, column_levels)]
    out = pl.pallas_call(
        functools.partial(kernel, nlon, levels, group),
        out_shape=jax.ShapeDtypeStruct((planes, rows, nlon), jnp.float32),
        in_specs=[hbm] * 3,
        out_specs=vmem,
        scratch_shapes=[
            f32(planes, rows, nlon),
            f32(*currents.shape),
            i32(*column_levels.shape),
            f32(rows, planes, width),
            f32(rows, planes, width),
            f32(rows, planes, width),
            f32(2, HALO, planes, whole),
            f32(2, HALO, planes, whole),
            f32(2, HALO, planes, whole),
            pack, pack, pack, pack,
            f32(2, rows, levels, nlon),
            f32(levels, nlon),
            f32(levels, nlon),
            i32(1, nlon), i32(1, nlon), i32(1, nlon), i32(1, nlon),
            f32(rows, 9, SUB, width),
            f32(6, SUB, width),
            f32(rows + 2, SUB, width),
            f32(2 * HALO, SUB, width),
            dma((chunks,)), dma((2,)),
        ] + [dma((2, chunks))] * 10 + [dma((4,)), dma((4,))],
        compiler_params=pltpu.CompilerParams(
            collective_id=0, has_side_effects=True, vmem_limit_bytes=44 * 1024 * 1024
        ),
    )(*args)
    return out.reshape(tracers.shape)


def layer_size(mesh):
    devices = mesh.devices.reshape(-1, mesh.shape["lat"])[0]
    spots = [getattr(d, "coords", None) for d in devices]
    if any(s is None or len(s) < 3 for s in spots):
        return 4
    return sum(s[2] == spots[0][2] for s in spots)


def solution(mesh):
    in_specs = (
        P("member", None, "lat", None),
        P("member", None, "lat", None),
        P(("member", "lat"), None),
    )
    out_specs = P("member", None, "lat", None)
    return jax.shard_map(
        functools.partial(shards, layer_size(mesh)),
        mesh=mesh, in_specs=in_specs, out_specs=out_specs, check_vma=False,
    )
```

profile of v0, /device:TPU:3, one launch (start us, length us, event | category | flops | bytes accessed | tf_op | source)
XLA Modules:
  0.0 72.9 jit_solution(4841647471166410703)
XLA Ops:
  0.0 71.3 %shard_map.37 = f32[120,4,1440]{2,1,0:T(4,128)S(1)} custom-call(f32[120,4,1440]{2,1,0:T(4,128)} %bitcast.3, f32[2,4,4,1440]{3,2,1,0:T(4,128)} %flow_hbm.1, s32[4,1440]{1,0:T(4,128)} %lev_hbm.1), custom_call_target="tpu_custom_call" | custom-call | tf_op jit(solution)/shard_map/pallas_call | solution.py:483
  71.3 1.6 %copy.5 = f32[30,4,4,1440]{3,2,1,0:T(4,128)} copy(f32[30,4,4,1440]{3,2,1,0:T(4,128)S(1)} %bitcast.2) | data formatting | bytes 5529600
where the time goes:
time: 73.1 us; the launch traced here: 72.9 us
  Pallas kernels  71.3 us (98%)
  local copies, waits for them, and re-layouts  1.6 us (2%)
    pallas_call x1, Pallas kernels, shards(): pl.pallas_call(functools.partial(kernel, nlon, levels, group), out_shape=...  71.3 us
    unnamed x1, local copies, waits for them, and re-layouts  1.6 us

commit v1 on v0

--- a/solution.py
+++ b/solution.py
@@ -11,6 +11,7 @@
 SUB = 8
 WRAP = 4
 HALO = 2
+LEAD = 6
 MESH = pl.DeviceIdType.MESH
 
 
@@ -54,15 +55,11 @@
 def mirrored(tiles, nlon):
     count = len(tiles)
     rest = nlon % LANES
-    row = lax.broadcasted_iota(jnp.int32, (LANES, LANES), 0)
-    col = lax.broadcasted_iota(jnp.int32, (LANES, LANES), 1)
-    near = jnp.where((row + col == rest - 1), 1.0, 0.0).astype(jnp.float32)
-    far = jnp.where((row + col == LANES + rest - 1), 1.0, 0.0).astype(jnp.float32)
-    dot = functools.partial(
-        jnp.dot, precision=lax.Precision.HIGHEST, preferred_element_type=jnp.float32
-    )
+    lane = lax.broadcasted_iota(jnp.int32, tiles[0].shape, 1)
+    source = jnp.where(lane < rest, rest - 1 - lane, LANES + rest - 1 - lane)
+    turned = [jnp.take_along_axis(t, source, axis=1, mode="promise_in_bounds") for t in tiles]
     return [
-        dot(tiles[(count - 1 - q) % count], near) + dot(tiles[(count - 2 - q) % count], far)
+        jnp.where(lane < rest, turned[(count - 1 - q) % count], turned[(count - 2 - q) % count])
         for q in range(count)
     ]
 
@@ -256,6 +253,20 @@
                     main(phase, up, g, True).wait_recv()
                     forward(phase, up, g).start()
 
+    lead = min(LEAD, chunks)
+
+    def pass_first(phase):
+        def one(g, carry):
+            pass_on(phase, g)
+            return carry
+
+        lax.fori_loop(0, lead, one, 0)
+
+    def pass_next(phase, g):
+        @pl.when(g + lead < chunks)
+        def _():
+            pass_on(phase, g + lead)
+
     def arrived(phase, g):
         for up, near in ((True, has_lo), (False, has_hi)):
             @pl.when(near)
@@ -286,19 +297,18 @@
     spans = [(q * LANES, min(LANES, nlon - q * LANES)) for q in range(width // LANES)]
 
     def tiles_of(x):
-        lane = lax.broadcasted_iota(jnp.int32, (x.shape[0], LANES), 1)
-        tiles = [x[:, q * LANES : (q + 1) * LANES] for q in range(width // LANES)]
-        return tiles[:-1] + [jnp.where(lane < rest, tiles[-1], 0.0)]
+        return [x[:, q * LANES : (q + 1) * LANES] for q in range(width // LANES)]
 
     def fold(phase, g):
         part = part_of(g)
         own = first if phase else start
-        x = jnp.concatenate([own[rows - 1 - k, part, :] for k in range(HALO)], axis=0)
-        tiles = mirrored(tiles_of(x), nlon)
-        for (at, n), t in zip(spans[:-1], tiles[:-1]):
-            for k in range(HALO):
-                hi[phase, k, part, at : at + n] = t[SUB * k : SUB * k + SUB]
-        pack_hi[phase, g] = packed(tiles[-1][:SUB], tiles[-1][SUB:], rest)
+        ends = []
+        for k in range(HALO):
+            tiles = mirrored(tiles_of(own[rows - 1 - k, part, :]), nlon)
+            for (at, n), t in zip(spans[:-1], tiles[:-1]):
+                hi[phase, k, part, at : at + n] = t
+            ends.append(tiles[-1])
+        pack_hi[phase, g] = packed(*ends, rest)
 
     @pl.when(jnp.logical_not(has_lo))
     def _():
@@ -391,7 +401,7 @@
         return total
 
     def step(g, carry):
-        pass_on(0, g)
+        pass_next(0, g)
         arrived(0, g)
         part = part_of(g)
         for low, mains, packs in ((0, lo, pack_lo), (HALO, hi, pack_hi)):
@@ -423,10 +433,11 @@
 
         return carry
 
+    pass_first(0)
     lax.fori_loop(0, chunks, step, 0)
 
     def last(g, carry):
-        pass_on(1, g)
+        pass_next(1, g)
         sent(0, g)
         arrived(1, g)
         part = part_of(g)
@@ -442,6 +453,7 @@
             out_ref[part, k, :] = value[:, :nlon]
         return carry
 
+    pass_first(1)
     lax.fori_loop(0, chunks, last, 0)
 
     @pl.when(has_hi)

time: 73.1 us -> 62.6 us (0.86)
  the two profiles are of different devices: /device:TPU:3 before, /device:TPU:9 now
where the time goes in v1:
time: 62.6 us; the launch traced here: 61.5 us
  Pallas kernels  59.9 us (96%)
  local copies, waits for them, and re-layouts  1.6 us (3%)
    pallas_call x1, Pallas kernels, shards(): pl.pallas_call(functools.partial(kernel, nlon, levels, group), out_shape=...  59.9 us
    unnamed x1, local copies, waits for them, and re-layouts  1.6 us

profile of v1, /device:TPU:9, one launch (start us, length us, event | category | flops | bytes accessed | tf_op | source)
XLA Modules:
  0.0 61.5 jit_solution(11482728244897016348)
XLA Ops:
  0.0 59.9 %shard_map.37 = f32[120,4,1440]{2,1,0:T(4,128)S(1)} custom-call(f32[120,4,1440]{2,1,0:T(4,128)} %bitcast.3, f32[2,4,4,1440]{3,2,1,0:T(4,128)} %flow_hbm.1, s32[4,1440]{1,0:T(4,128)} %lev_hbm.1), custom_call_target="tpu_custom_call" | custom-call | tf_op jit(solution)/shard_map/pallas_call | solution.py:495
  59.9 1.6 %copy.5 = f32[30,4,4,1440]{3,2,1,0:T(4,128)} copy(f32[30,4,4,1440]{3,2,1,0:T(4,128)S(1)} %bitcast.2) | data formatting | bytes 5529600

commit v2 on v1

--- a/solution.py
+++ b/solution.py
@@ -11,7 +11,9 @@
 SUB = 8
 WRAP = 4
 HALO = 2
-LEAD = 6
+LEAD = 2
+WIDEST = 3
+PACK_CUT = 3
 MESH = pl.DeviceIdType.MESH
 
 
@@ -64,8 +66,37 @@
     ]
 
 
+def growing(n):
+    sizes, step = [], 1
+    while sum(sizes) < n:
+        sizes.append(min(step, n - sum(sizes)))
+        step = min(2 * step, WIDEST)
+    return sizes
+
+
+def spans_of(sizes):
+    return [(sum(sizes[:i]), n) for i, n in enumerate(sizes)]
+
+
+def detours(sizes, layers):
+    names = [(phase, i) for phase in range(2) for i in range(len(sizes[phase]))][:-1]
+    result = []
+    for share in range(layers):
+        goal = sum(sizes[0] + sizes[1]) * share / layers
+        best = None
+        for bits in range(2 ** len(names)):
+            chosen = [name for n, name in enumerate(names) if bits >> n & 1]
+            load = [sum(sizes[p][i] for p, i in chosen if p == phase) for phase in range(2)]
+            late = sum(i for _, i in chosen)
+            cost = (abs(sum(load) - goal), abs(load[0] - goal / 2), late)
+            if best is None or cost < best[0]:
+                best = (cost, chosen)
+        result.append(best[1])
+    return result
+
+
 def kernel(
-    nlon, levels, group, raw_hbm, flow_hbm, lev_hbm, out_ref,
+    nlon, levels, group, sizes, raw_hbm, flow_hbm, lev_hbm, out_ref,
     raw, raw_flow, lev_ref, start, first, partial, lo, hi, relay, pack_up, pack_dn, pack_lo, pack_hi,
     flow, v_lo, v_hi, lev_up, lev_dn, lev_lo, lev_hi, coef, edge, wets, halo,
     load, aux_load, send_up, send_dn, recv_lo, recv_hi, relay_in, relay_out,
@@ -77,6 +108,9 @@
     rest = nlon % LANES
     whole = nlon - rest
     chunks = planes // SUB
+    groups = [spans_of(x) for x in sizes]
+    cut = min(PACK_CUT, chunks - 1)
+    packs = [[(0, cut), (cut, chunks - cut)], [(0, chunks - cut), (chunks - cut, cut)]]
     layers = lat // group
     layer = me // group
     place = me % group
@@ -99,9 +133,10 @@
     def part_of(g):
         return pl.ds(pl.multiple_of(g * SUB, SUB), SUB)
 
-    def loading(g):
-        part = part_of(g)
-        return pltpu.make_async_copy(raw_hbm.at[part], raw.at[part], load.at[g])
+    def loading(i):
+        at, n = groups[0][i]
+        part = pl.ds(at * SUB, n * SUB)
+        return pltpu.make_async_copy(raw_hbm.at[part], raw.at[part], load.at[i])
 
     lev_load = pltpu.make_async_copy(lev_hbm, lev_ref, aux_load.at[0])
     flow_load = pltpu.make_async_copy(flow_hbm, raw_flow, aux_load.at[1])
@@ -114,11 +149,8 @@
         def _(by=by):
             pl.semaphore_signal(barrier, inc=1, device_id={"lat": me + by}, device_id_type=MESH)
 
-    def load_rest(g, carry):
-        loading(g).start()
-        return carry
-
-    lax.fori_loop(1, chunks, load_rest, 0)
+    for i in range(1, len(groups[0])):
+        loading(i).start()
 
     ranks = lax.rem(lax.broadcasted_iota(jnp.int32, (SUB, nlon), 0), levels)
 
@@ -138,14 +170,14 @@
 
     def reorder(g):
         part = part_of(g)
-        loading(g).wait()
-        tails = []
+        ends = []
         for k in range(rows):
             x = wrapped(raw[part, k, :], nlon) * wets[k + 1]
             start[k, part, :] = x
-            tails.append(x[:, whole:])
-        put_packs(0, g, lambda k: tails[k])
-
+            ends.append(x[:, whole:])
+        put_packs(0, g, lambda k: ends[k])
+
+    loading(0).wait()
     reorder(0)
     flow_load.wait()
     for k in range(rows):
@@ -172,107 +204,127 @@
             for i, (src, dst) in enumerate(pieces)
         ]
 
-    def main(phase, up, g, via):
-        part = part_of(g)
+    def main(phase, up, i, via=False):
+        at, n = (0, chunks) if i is None else groups[phase][i]
+        part = pl.ds(at * SUB, n * SUB)
         own = first if phase else start
         src = own.at[pl.ds(rows - HALO if up else 0, HALO), part, pl.ds(0, whole)]
-        s = (send_up if up else send_dn).at[phase, g]
+        s = (send_up if up else send_dn).at[phase]
+        i = i or 0
         if via:
             by = 1 - group if up else group - 1
-            return remote(src, relay.at[phase, :, part], s, relay_in.at[phase, g], by)
+            return remote(src, relay.at[phase, :, part], s, relay_in.at[phase, i], by)
         dst = (lo if up else hi).at[phase, :, part]
-        r = (recv_lo if up else recv_hi).at[phase, g]
+        r = (recv_lo if up else recv_hi).at[phase, i]
         return remote(src, dst, s, r, 1 if up else -1)
 
-    def tails(phase, up, g):
+    def ends_copy(phase, up, i):
+        at, n = (0, chunks) if i is None else packs[phase][i]
+        part = pl.ds(at, n)
+        i = i or 0
         if up:
-            return remote(pack_up.at[phase, g], pack_lo.at[phase, g],
-                          psend_up.at[phase, g], precv_lo.at[phase, g], 1)
-        return remote(pack_dn.at[phase, g], pack_hi.at[phase, g],
-                      psend_dn.at[phase, g], precv_hi.at[phase, g], -1)
-
-    def forward(phase, up, g):
-        part = part_of(g)
+            return remote(pack_up.at[phase, part], pack_lo.at[phase, part],
+                          psend_up.at[phase], precv_lo.at[phase, i], 1)
+        return remote(pack_dn.at[phase, part], pack_hi.at[phase, part],
+                      psend_dn.at[phase], precv_hi.at[phase, i], -1)
+
+    def forward(phase, up, i):
+        at, n = groups[phase][i]
+        part = pl.ds(at * SUB, n * SUB)
         dst = (lo if up else hi).at[phase, :, part]
-        r = (recv_lo if up else recv_hi).at[phase, g]
-        return remote(relay.at[phase, :, part], dst, relay_out.at[phase, g], r,
+        r = (recv_lo if up else recv_hi).at[phase, i]
+        return remote(relay.at[phase, :, part], dst, relay_out.at[phase, i], r,
                       group if up else -group)
 
-    def detour(share, phase, g):
-        left = chunks - 1 - g
-        shift = 1 - phase
-        return ((left + 1) * share + shift) // layers - (left * share + shift) // layers == 1
-
-    def detour_up(phase, g):
-        return detour(layers - 1 - layer, phase, g)
-
-    def detour_dn(phase, g):
-        return detour(layer, phase, g)
-
-    def send(phase, g):
-        for up, near, end, bent in (
-            (True, has_hi, is_last, detour_up), (False, has_lo, is_first, detour_dn),
-        ):
-            if relays:
-                by_relay = near & end & bent(phase, g)
+    table = detours(sizes, layers) if relays else []
+
+    def bent(phase, i, share):
+        result = False
+        for value, chosen in enumerate(table):
+            if (phase, i) in chosen:
+                result = result | (share == value)
+        return result
+
+    bent_up = {(p, i): bent(p, i, layers - 1 - layer) for p in range(2) for i in range(len(sizes[p]))}
+    bent_dn = {(p, i): bent(p, i, layer) for p in range(2) for i in range(len(sizes[p]))}
+    ways = ((True, has_hi, is_last, bent_up), (False, has_lo, is_first, bent_dn))
+    duties = ((True, is_first, bent_up), (False, is_last, bent_dn))
+
+    def send(phase, i):
+        for up, near, end, flags in ways:
+            flag = flags[phase, i]
+            if flag is False:
+                @pl.when(near)
+                def _(up=up):
+                    main(phase, up, i).start()
+            else:
+                by_relay = near & end & flag
 
                 @pl.when(by_relay)
                 def _(up=up):
-                    main(phase, up, g, True).start()
+                    main(phase, up, i, True).start()
 
                 @pl.when(near & jnp.logical_not(by_relay))
                 def _(up=up):
-                    main(phase, up, g, False).start()
-            else:
-                @pl.when(near)
-                def _(up=up):
-                    main(phase, up, g, False).start()
-
+                    main(phase, up, i).start()
+
+    def send_ends(phase, i):
+        for up, near, _, _ in ways:
             @pl.when(near)
             def _(up=up):
-                tails(phase, up, g).start()
-
-    def sent(phase, g):
-        for up, near in ((True, has_hi), (False, has_lo)):
-            @pl.when(near)
-            def _(up=up):
-                main(phase, up, g, False).wait_send()
-                tails(phase, up, g).wait_send()
-
-        if relays:
-            for up, end, bent in ((True, is_first, detour_up), (False, is_last, detour_dn)):
-                @pl.when(end & bent(phase, g))
+                ends_copy(phase, up, i).start()
+
+    def pass_on(phase, i):
+        for up, end, flags in duties:
+            flag = flags[phase, i]
+            if flag is not False:
+                @pl.when(end & flag)
                 def _(up=up):
-                    forward(phase, up, g).wait_send()
-
-    def pass_on(phase, g):
-        if relays:
-            for up, end, bent in ((True, is_first, detour_up), (False, is_last, detour_dn)):
-                @pl.when(end & bent(phase, g))
+                    main(phase, up, i, True).wait_recv()
+                    forward(phase, up, i).start()
+
+    def passed(phase, i):
+        for up, end, flags in duties:
+            flag = flags[phase, i]
+            if flag is not False:
+                @pl.when(end & flag)
                 def _(up=up):
-                    main(phase, up, g, True).wait_recv()
-                    forward(phase, up, g).start()
-
-    lead = min(LEAD, chunks)
-
-    def pass_first(phase):
-        def one(g, carry):
-            pass_on(phase, g)
-            return carry
-
-        lax.fori_loop(0, lead, one, 0)
-
-    def pass_next(phase, g):
-        @pl.when(g + lead < chunks)
-        def _():
-            pass_on(phase, g + lead)
-
-    def arrived(phase, g):
+                    forward(phase, up, i).wait_send()
+
+    def arrived(copy, phase, i):
         for up, near in ((True, has_lo), (False, has_hi)):
             @pl.when(near)
             def _(up=up):
-                main(phase, up, g, False).wait_recv()
-                tails(phase, up, g).wait_recv()
+                copy(phase, up, i).wait_recv()
+
+    def receive(phase, g):
+        for i, (at, _) in enumerate(groups[phase]):
+            @pl.when(g == at)
+            def _(i=i):
+                if i == 0:
+                    for j in range(min(LEAD, len(groups[phase]))):
+                        pass_on(phase, j)
+                if i + LEAD < len(groups[phase]):
+                    pass_on(phase, i + LEAD)
+                arrived(main, phase, i)
+
+        for i, (at, _) in enumerate(packs[phase]):
+            @pl.when(g == at)
+            def _(i=i):
+                arrived(ends_copy, phase, i)
+
+    def dispatch(phase, g):
+        for i, (at, n) in enumerate(groups[phase]):
+            @pl.when(g == at + n - 1)
+            def _(i=i):
+                send(phase, i)
+
+        for i, (at, n) in enumerate(packs[phase]):
+            @pl.when(g == at + n - 1)
+            def _(i=i):
+                send_ends(phase, i)
+
+    send(0, 0)
 
     @pl.when(has_hi)
     def _():
@@ -285,14 +337,22 @@
             c.start()
 
     def begin(g, carry):
-        @pl.when(g < chunks - 1)
+        for i, (at, _) in enumerate(groups[0]):
+            if i:
+                @pl.when(g == at)
+                def _(i=i):
+                    loading(i).wait()
+
+        reorder(g)
+
+        @pl.when(g > 1)
         def _():
-            reorder(g + 1)
-
-        send(0, g)
+            dispatch(0, g - 1)
+
         return carry
 
-    lax.fori_loop(0, chunks, begin, 0)
+    lax.fori_loop(1, chunks, begin, 0)
+    dispatch(0, chunks - 1)
 
     spans = [(q * LANES, min(LANES, nlon - q * LANES)) for q in range(width // LANES)]
 
@@ -401,11 +461,10 @@
         return total
 
     def step(g, carry):
-        pass_next(0, g)
-        arrived(0, g)
+        receive(0, g)
         part = part_of(g)
-        for low, mains, packs in ((0, lo, pack_lo), (HALO, hi, pack_hi)):
-            for k, t in enumerate(unpacked(packs[0, g], rest)):
+        for low, mains, ends in ((0, lo, pack_lo), (HALO, hi, pack_hi)):
+            for k, t in enumerate(unpacked(ends[0, g], rest)):
                 halo[low + k] = joined(mains[0, k, part, :], t, rest)
 
         def field(j):
@@ -425,7 +484,7 @@
         for k in range(rows):
             partial[k, part, :] = 0.5 * (start[k, part, :] * wets[k + 1] + section(own, k))
 
-        send(1, g)
+        dispatch(1, g)
 
         @pl.when(jnp.logical_not(has_hi))
         def _():
@@ -433,17 +492,14 @@
 
         return carry
 
-    pass_first(0)
     lax.fori_loop(0, chunks, step, 0)
 
     def last(g, carry):
-        pass_next(1, g)
-        sent(0, g)
-        arrived(1, g)
+        receive(1, g)
         part = part_of(g)
         others = {}
-        for low, mains, packs in ((-HALO, lo, pack_lo), (rows, hi, pack_hi)):
-            for k, t in enumerate(unpacked(packs[1, g], rest)):
+        for low, mains, ends in ((-HALO, lo, pack_lo), (rows, hi, pack_hi)):
+            for k, t in enumerate(unpacked(ends[1, g], rest)):
                 others[low + k] = jnp.concatenate([mains[1, k, part, :], t], axis=1)
         for k in range(rows):
             value = partial[k, part, :]
@@ -453,24 +509,20 @@
             out_ref[part, k, :] = value[:, :nlon]
         return carry
 
-    pass_first(1)
     lax.fori_loop(0, chunks, last, 0)
 
-    @pl.when(has_hi)
-    def _():
-        for c in flows(True):
-            c.wait_send()
-
-    @pl.when(has_lo)
-    def _():
-        for c in flows(False):
-            c.wait_send()
-
-    def finish(g, carry):
-        sent(1, g)
-        return carry
-
-    lax.fori_loop(0, chunks, finish, 0)
+    for up, near, _, _ in ways:
+        @pl.when(near)
+        def _(up=up):
+            for c in flows(up):
+                c.wait_send()
+            for phase in range(2):
+                main(phase, up, None).wait_send()
+                ends_copy(phase, up, None).wait_send()
+
+    for phase in range(2):
+        for i in range(len(groups[phase])):
+            passed(phase, i)
 
 
 def shards(group, tracers, currents, column_levels):
@@ -480,6 +532,8 @@
     whole = nlon - nlon % LANES
     raw = tracers.reshape(planes, rows, nlon)
     chunks = planes // SUB
+    sizes = [growing(chunks), growing(chunks)[::-1]]
+    count = len(sizes[0])
     hbm = pl.BlockSpec(memory_space=pltpu.HBM)
     vmem = pl.BlockSpec(memory_space=pltpu.VMEM)
     dma = pltpu.SemaphoreType.DMA
@@ -493,7 +547,7 @@
     pack = f32(2, chunks, SUB // 2, LANES)
     args = [pltpu.with_memory_space_constraint(x, pltpu.HBM) for x in (raw, currents, column_levels)]
     out = pl.pallas_call(
-        functools.partial(kernel, nlon, levels, group),
+        functools.partial(kernel, nlon, levels, group, sizes),
         out_shape=jax.ShapeDtypeStruct((planes, rows, nlon), jnp.float32),
         in_specs=[hbm] * 3,
         out_specs=vmem,
@@ -516,8 +570,10 @@
             f32(6, SUB, width),
             f32(rows + 2, SUB, width),
             f32(2 * HALO, SUB, width),
-            dma((chunks,)), dma((2,)),
-        ] + [dma((2, chunks))] * 10 + [dma((4,)), dma((4,))],
+            dma((count,)), dma((2,)), dma((2,)), dma((2,)),
+            dma((2, count)), dma((2, count)), dma((2, count)), dma((2, count)),
+            dma((2,)), dma((2,)), dma((2, 2)), dma((2, 2)), dma((4,)), dma((4,)),
+        ],
         compiler_params=pltpu.CompilerParams(
             collective_id=0, has_side_effects=True, vmem_limit_bytes=44 * 1024 * 1024
         ),

time: 62.6 us -> 60.7 us (0.970); the launches traced: 61.5 us -> 60.4 us
  Pallas kernels: 59.9 us -> 58.8 us
    pallas_call x1, Pallas kernels: 59.9 us -> 58.8 us  [shards(): pl.pallas_call(functools.partial(kernel, nlon, levels, group, sizes), out...]
where the time goes in v2:
time: 60.7 us; the launch traced here: 60.4 us
  Pallas kernels  58.8 us (97%)
  local copies, waits for them, and re-layouts  1.6 us (3%)
    pallas_call x1, Pallas kernels, shards(): pl.pallas_call(functools.partial(kernel, nlon, levels, group, sizes), out...  58.8 us
    unnamed x1, local copies, waits for them, and re-layouts  1.6 us

profile of v2, /device:TPU:9, one launch (start us, length us, event | category | flops | bytes accessed | tf_op | source)
XLA Modules:
  0.0 60.4 jit_solution(16982261978369979709)
XLA Ops:
  0.0 58.8 %shard_map.37 = f32[120,4,1440]{2,1,0:T(4,128)S(1)} custom-call(f32[120,4,1440]{2,1,0:T(4,128)} %bitcast.3, f32[2,4,4,1440]{3,2,1,0:T(4,128)} %flow_hbm.1, s32[4,1440]{1,0:T(4,128)} %lev_hbm.1), custom_call_target="tpu_custom_call" | custom-call | tf_op jit(solution)/shard_map/pallas_call | solution.py:549
  58.8 1.6 %copy.5 = f32[30,4,4,1440]{3,2,1,0:T(4,128)} copy(f32[30,4,4,1440]{3,2,1,0:T(4,128)S(1)} %bitcast.2) | data formatting | bytes 5529600

commit v3 on v2

--- a/solution.py
+++ b/solution.py
@@ -11,9 +11,10 @@
 SUB = 8
 WRAP = 4
 HALO = 2
-LEAD = 2
-WIDEST = 3
+LEAD = 3
+WIDEST = 2
 PACK_CUT = 3
+AHEAD = 2
 MESH = pl.DeviceIdType.MESH
 
 
@@ -66,11 +67,11 @@
     ]
 
 
-def growing(n):
-    sizes, step = [], 1
+def growing(n, step):
+    sizes = []
     while sum(sizes) < n:
         sizes.append(min(step, n - sum(sizes)))
-        step = min(2 * step, WIDEST)
+        step = min(step + 1, WIDEST)
     return sizes
 
 
@@ -79,7 +80,7 @@
 
 
 def detours(sizes, layers):
-    names = [(phase, i) for phase in range(2) for i in range(len(sizes[phase]))][:-1]
+    names = [(phase, i) for phase in range(2) for i in range(len(sizes[phase]))][1:-2]
     result = []
     for share in range(layers):
         goal = sum(sizes[0] + sizes[1]) * share / layers
@@ -97,10 +98,10 @@
 
 def kernel(
     nlon, levels, group, sizes, raw_hbm, flow_hbm, lev_hbm, out_ref,
-    raw, raw_flow, lev_ref, start, first, partial, lo, hi, relay, pack_up, pack_dn, pack_lo, pack_hi,
-    flow, v_lo, v_hi, lev_up, lev_dn, lev_lo, lev_hi, coef, edge, wets, halo,
+    raw, raw_flow, lev_ref, raw_lo, raw_hi, start, first, partial, lo, hi, relay, pack_up, pack_dn, pack_lo, pack_hi,
+    flow, v_lo, v_hi, lev_lo, lev_hi, coef, edge, wets, halo,
     load, aux_load, send_up, send_dn, recv_lo, recv_hi, relay_in, relay_out,
-    psend_up, psend_dn, precv_lo, precv_hi, fsend, frecv,
+    psend_up, psend_dn, precv_lo, precv_hi, fsend, frecv, send_raw,
 ):
     lat = lax.axis_size("lat")
     me = lax.axis_index("lat")
@@ -140,51 +141,17 @@
 
     lev_load = pltpu.make_async_copy(lev_hbm, lev_ref, aux_load.at[0])
     flow_load = pltpu.make_async_copy(flow_hbm, raw_flow, aux_load.at[1])
-    lev_load.start()
-    loading(0).start()
-    flow_load.start()
-
     for near, by in pairs:
         @pl.when(near)
         def _(by=by):
             pl.semaphore_signal(barrier, inc=1, device_id={"lat": me + by}, device_id_type=MESH)
 
+    lev_load.start()
+    loading(0).start()
+    flow_load.start()
+
     for i in range(1, len(groups[0])):
         loading(i).start()
-
-    ranks = lax.rem(lax.broadcasted_iota(jnp.int32, (SUB, nlon), 0), levels)
-
-    def wet_of(row):
-        lev = jnp.broadcast_to(row, (SUB, nlon))
-        return wrapped(jnp.where(ranks < lev, 1.0, 0.0), nlon)
-
-    lev_load.wait()
-    for k in range(rows):
-        wets[k + 1] = wet_of(lev_ref[k : k + 1, :])
-    lev_up[...] = lev_ref[rows - 1 : rows, :]
-    lev_dn[...] = lev_ref[0:1, :]
-
-    def put_packs(phase, g, tail):
-        pack_up[phase, g] = packed(tail(rows - 2), tail(rows - 1), rest)
-        pack_dn[phase, g] = packed(tail(0), tail(1), rest)
-
-    def reorder(g):
-        part = part_of(g)
-        ends = []
-        for k in range(rows):
-            x = wrapped(raw[part, k, :], nlon) * wets[k + 1]
-            start[k, part, :] = x
-            ends.append(x[:, whole:])
-        put_packs(0, g, lambda k: ends[k])
-
-    loading(0).wait()
-    reorder(0)
-    flow_load.wait()
-    for k in range(rows):
-        for which in range(2):
-            flow[which, k] = raw_flow[which, :, k, :]
-
-    pl.semaphore_wait(barrier, sum(jnp.where(near, 1, 0) for near, _ in pairs))
 
     def remote(src, dst, s, r, by):
         return pltpu.make_async_remote_copy(
@@ -194,18 +161,24 @@
 
     def flows(up):
         n = 0 if up else 2
-        if up:
-            pieces = [(flow.at[1, rows - 1], v_lo), (lev_up, lev_lo)]
-        else:
-            pieces = [(flow.at[1, 0], v_hi), (lev_dn, lev_hi)]
+        k = rows - 1 if up else 0
+        levs = lev_hbm.at[pl.ds(rows - HALO if up else 0, HALO)]
+        pieces = [(flow_hbm.at[1, :, k], v_lo if up else v_hi), (levs, lev_lo if up else lev_hi)]
         by = 1 if up else -1
         return [
             remote(src, dst, fsend.at[n + i], frecv.at[n + i], by)
             for i, (src, dst) in enumerate(pieces)
         ]
 
+    def unmasked(up):
+        n = groups[0][0][1] * SUB
+        src = raw_hbm.at[pl.ds(0, n), pl.ds(rows - HALO if up else 0, HALO), pl.ds(0, whole)]
+        s, r = (send_raw.at[0], recv_lo.at[0, 0]) if up else (send_raw.at[1], recv_hi.at[0, 0])
+        return remote(src, raw_lo if up else raw_hi, s, r, 1 if up else -1)
+
     def main(phase, up, i, via=False):
-        at, n = (0, chunks) if i is None else groups[phase][i]
+        skip = 0 if phase else groups[0][0][1]
+        at, n = (skip, chunks - skip) if i is None else groups[phase][i]
         part = pl.ds(at * SUB, n * SUB)
         own = first if phase else start
         src = own.at[pl.ds(rows - HALO if up else 0, HALO), part, pl.ds(0, whole)]
@@ -233,7 +206,7 @@
         part = pl.ds(at * SUB, n * SUB)
         dst = (lo if up else hi).at[phase, :, part]
         r = (recv_lo if up else recv_hi).at[phase, i]
-        return remote(relay.at[phase, :, part], dst, relay_out.at[phase, i], r,
+        return remote(relay.at[phase, :, part], dst, relay_out.at[phase], r,
                       group if up else -group)
 
     table = detours(sizes, layers) if relays else []
@@ -275,6 +248,8 @@
                 ends_copy(phase, up, i).start()
 
     def pass_on(phase, i):
+        if i:
+            passed(phase, i - 1)
         for up, end, flags in duties:
             flag = flags[phase, i]
             if flag is not False:
@@ -306,7 +281,7 @@
                         pass_on(phase, j)
                 if i + LEAD < len(groups[phase]):
                     pass_on(phase, i + LEAD)
-                arrived(main, phase, i)
+                arrived(main if phase or i else lambda phase, up, i: unmasked(up), phase, i)
 
         for i, (at, _) in enumerate(packs[phase]):
             @pl.when(g == at)
@@ -315,26 +290,54 @@
 
     def dispatch(phase, g):
         for i, (at, n) in enumerate(groups[phase]):
-            @pl.when(g == at + n - 1)
-            def _(i=i):
-                send(phase, i)
+            if phase or i:
+                @pl.when(g == at + n - 1)
+                def _(i=i):
+                    send(phase, i)
 
         for i, (at, n) in enumerate(packs[phase]):
             @pl.when(g == at + n - 1)
             def _(i=i):
                 send_ends(phase, i)
 
-    send(0, 0)
-
-    @pl.when(has_hi)
-    def _():
-        for c in flows(True):
-            c.start()
-
-    @pl.when(has_lo)
-    def _():
-        for c in flows(False):
-            c.start()
+    pl.semaphore_wait(barrier, sum(jnp.where(near, 1, 0) for near, _ in pairs))
+
+    for up, near, _, _ in ways:
+        @pl.when(near)
+        def _(up=up):
+            unmasked(up).start()
+            for c in flows(up):
+                c.start()
+
+    ranks = lax.rem(lax.broadcasted_iota(jnp.int32, (SUB, nlon), 0), levels)
+
+    def wet_of(row):
+        lev = jnp.broadcast_to(row, (SUB, nlon))
+        return wrapped(jnp.where(ranks < lev, 1.0, 0.0), nlon)
+
+    lev_load.wait()
+    for k in range(rows):
+        wets[k + 1] = wet_of(lev_ref[k : k + 1, :])
+
+    def put_packs(phase, g, tail):
+        pack_up[phase, g] = packed(tail(rows - 2), tail(rows - 1), rest)
+        pack_dn[phase, g] = packed(tail(0), tail(1), rest)
+
+    def reorder(g):
+        part = part_of(g)
+        ends = []
+        for k in range(rows):
+            x = wrapped(raw[part, k, :], nlon) * wets[k + 1]
+            start[k, part, :] = x
+            ends.append(x[:, whole:])
+        put_packs(0, g, lambda k: ends[k])
+
+    loading(0).wait()
+    reorder(0)
+    flow_load.wait()
+    for k in range(rows):
+        for which in range(2):
+            flow[which, k] = raw_flow[which, :, k, :]
 
     def begin(g, carry):
         for i, (at, _) in enumerate(groups[0]):
@@ -384,7 +387,7 @@
         x = jnp.concatenate([x, jnp.zeros((SUB, width - nlon), jnp.float32)], axis=1)
         for (at, n), t in zip(spans, mirrored(tiles_of(x), nlon)):
             v_hi[:, at : at + n] = -t[:levels, :n]
-            lev_hi[:, at : at + n] = (t[levels : levels + 1, :n] + 0.5).astype(jnp.int32)
+            lev_hi[0:1, at : at + n] = (t[levels : levels + 1, :n] + 0.5).astype(jnp.int32)
 
         def fold_start(g, carry):
             fold(0, g)
@@ -405,8 +408,8 @@
     def shift(x, by):
         return pltpu.roll(x, (-by) % width, 1)
 
-    wets[0] = wet_of(lev_lo[...])
-    wets[rows + 1] = wet_of(lev_hi[...])
+    wets[0] = wet_of(lev_lo[HALO - 1 : HALO, :])
+    wets[rows + 1] = wet_of(lev_hi[0:1, :])
 
     def spread(x):
         return wrapped(jnp.concatenate([x] * (SUB // levels), axis=0), nlon)
@@ -460,8 +463,22 @@
                 total += coef[k, 4 + i] * other
         return total
 
+    def mask_first(g):
+        part = part_of(g)
+        for near, source, levs, mains in ((has_lo, raw_lo, lev_lo, lo), (has_hi, raw_hi, lev_hi, hi)):
+            @pl.when(near)
+            def _(source=source, levs=levs, mains=mains):
+                for k in range(HALO):
+                    wet = jnp.where(ranks < jnp.broadcast_to(levs[k : k + 1, :], (SUB, nlon)), 1.0, 0.0)
+                    mains[0, k, part, :] = source[part, k, :] * wet[:, :whole]
+
     def step(g, carry):
         receive(0, g)
+
+        @pl.when(g < groups[0][0][1])
+        def _():
+            mask_first(g)
+
         part = part_of(g)
         for low, mains, ends in ((0, lo, pack_lo), (HALO, hi, pack_hi)):
             for k, t in enumerate(unpacked(ends[0, g], rest)):
@@ -514,15 +531,14 @@
     for up, near, _, _ in ways:
         @pl.when(near)
         def _(up=up):
-            for c in flows(up):
+            for c in [unmasked(up)] + flows(up):
                 c.wait_send()
             for phase in range(2):
                 main(phase, up, None).wait_send()
                 ends_copy(phase, up, None).wait_send()
 
     for phase in range(2):
-        for i in range(len(groups[phase])):
-            passed(phase, i)
+        passed(phase, len(groups[phase]) - 1)
 
 
 def shards(group, tracers, currents, column_levels):
@@ -532,8 +548,8 @@
     whole = nlon - nlon % LANES
     raw = tracers.reshape(planes, rows, nlon)
     chunks = planes // SUB
-    sizes = [growing(chunks), growing(chunks)[::-1]]
-    count = len(sizes[0])
+    sizes = [growing(chunks, AHEAD), growing(chunks, 1)[::-1]]
+    count = max(map(len, sizes))
     hbm = pl.BlockSpec(memory_space=pltpu.HBM)
     vmem = pl.BlockSpec(memory_space=pltpu.VMEM)
     dma = pltpu.SemaphoreType.DMA
@@ -555,6 +571,8 @@
             f32(planes, rows, nlon),
             f32(*currents.shape),
             i32(*column_levels.shape),
+            f32(sizes[0][0] * SUB, HALO, whole),
+            f32(sizes[0][0] * SUB, HALO, whole),
             f32(rows, planes, width),
             f32(rows, planes, width),
             f32(rows, planes, width),
@@ -565,14 +583,14 @@
             f32(2, rows, levels, nlon),
             f32(levels, nlon),
             f32(levels, nlon),
-            i32(1, nlon), i32(1, nlon), i32(1, nlon), i32(1, nlon),
+            i32(HALO, nlon), i32(HALO, nlon),
             f32(rows, 9, SUB, width),
             f32(6, SUB, width),
             f32(rows + 2, SUB, width),
             f32(2 * HALO, SUB, width),
-            dma((count,)), dma((2,)), dma((2,)), dma((2,)),
-            dma((2, count)), dma((2, count)), dma((2, count)), dma((2, count)),
-            dma((2,)), dma((2,)), dma((2, 2)), dma((2, 2)), dma((4,)), dma((4,)),
+            dma((len(sizes[0]),)), dma((2,)), dma((2,)), dma((2,)),
+            dma((2, count)), dma((2, count)), dma((2, count)), dma((2,)),
+            dma((2,)), dma((2,)), dma((2, 2)), dma((2, 2)), dma((4,)), dma((4,)), dma((2,)),
         ],
         compiler_params=pltpu.CompilerParams(
             collective_id=0, has_side_effects=True, vmem_limit_bytes=44 * 1024 * 1024

time: 60.7 us -> 59.7 us (0.984); the launches traced: 60.4 us -> 58.6 us
  Pallas kernels: 58.8 us -> 57 us
    pallas_call x1, Pallas kernels: 58.8 us -> 57 us  [shards(): pl.pallas_call(functools.partial(kernel, nlon, levels, group, sizes), out...]
where the time goes in v3:
time: 59.7 us; the launch traced here: 58.6 us
  Pallas kernels  57 us (95%)
  local copies, waits for them, and re-layouts  1.6 us (3%)
    pallas_call x1, Pallas kernels, shards(): pl.pallas_call(functools.partial(kernel, nlon, levels, group, sizes), out...  57 us
    unnamed x1, local copies, waits for them, and re-layouts  1.6 us

profile of v3, /device:TPU:9, one launch (start us, length us, event | category | flops | bytes accessed | tf_op | source)
XLA Modules:
  0.0 58.6 jit_solution(13601439289938764615)
XLA Ops:
  0.0 57.0 %shard_map.37 = f32[120,4,1440]{2,1,0:T(4,128)S(1)} custom-call(f32[120,4,1440]{2,1,0:T(4,128)} %bitcast.3, f32[2,4,4,1440]{3,2,1,0:T(4,128)} %flow_hbm.1, s32[4,1440]{1,0:T(4,128)} %lev_hbm.1), custom_call_target="tpu_custom_call" | custom-call | tf_op jit(solution)/shard_map/pallas_call | solution.py:565
  57.0 1.6 %copy.5 = f32[30,4,4,1440]{3,2,1,0:T(4,128)} copy(f32[30,4,4,1440]{3,2,1,0:T(4,128)S(1)} %bitcast.2) | data formatting | bytes 5529600

commit v4 on v3

--- a/solution.py
+++ b/solution.py
@@ -11,10 +11,12 @@
 SUB = 8
 WRAP = 4
 HALO = 2
-LEAD = 3
-WIDEST = 2
+LEAD = 2, 1
+WIDEST = 4
 PACK_CUT = 3
 AHEAD = 2
+KEEP = 2
+DIRECT = 0.0
 MESH = pl.DeviceIdType.MESH
 
 
@@ -79,25 +81,52 @@
     return [(sum(sizes[:i]), n) for i, n in enumerate(sizes)]
 
 
-def detours(sizes, layers):
-    names = [(phase, i) for phase in range(2) for i in range(len(sizes[phase]))][1:-2]
+def load_sizes(chunks):
+    rest = chunks - AHEAD
+    return [AHEAD, rest // 3, rest - rest // 3]
+
+
+def pack_sizes(chunks):
+    early = [PACK_CUT]
+    while sum(early) < chunks:
+        early.append(min(PACK_CUT + 1, chunks - sum(early)))
+    return [early, early[::-1]]
+
+
+def pieces_of(chunks):
+    sizes = [AHEAD, 1] + growing(chunks - AHEAD - 3, WIDEST) + [1, 1]
+    early = [(at, n, 0, HALO) for at, n in spans_of(sizes)]
+    at, n, _, _ = early.pop()
+    early += [(at, n, k, 1) for k in range(HALO)]
+    late = [(at, n, 0, HALO) for at, n in spans_of(growing(chunks, 1)[::-1])]
+    return [early, late]
+
+
+def subsets(items):
+    best = {0: []}
+    for size, name in items:
+        for total, chosen in list(best.items()):
+            best.setdefault(total + size, chosen + [name])
+    return best
+
+
+def detours(groups, layers):
+    size = {(p, i): n * k / HALO for p in range(2) for i, (_, n, _, k) in enumerate(groups[p])}
+    names = list(size)[1:-KEEP]
+    choices = [subsets([(size[n], n) for n in names if n[0] == phase]) for phase in range(2)]
     result = []
     for share in range(layers):
-        goal = sum(sizes[0] + sizes[1]) * share / layers
-        best = None
-        for bits in range(2 ** len(names)):
-            chosen = [name for n, name in enumerate(names) if bits >> n & 1]
-            load = [sum(sizes[p][i] for p, i in chosen if p == phase) for phase in range(2)]
-            late = sum(i for _, i in chosen)
-            cost = (abs(sum(load) - goal), abs(load[0] - goal / 2), late)
-            if best is None or cost < best[0]:
-                best = (cost, chosen)
-        result.append(best[1])
+        goal = (sum(size.values()) + DIRECT) * share / layers
+        _, one, two = min(
+            ((abs(one + two - goal), abs(one - goal / 2)), one, two)
+            for one in choices[0] for two in choices[1]
+        )
+        result.append(choices[0][one] + choices[1][two] if share else [])
     return result
 
 
 def kernel(
-    nlon, levels, group, sizes, raw_hbm, flow_hbm, lev_hbm, out_ref,
+    nlon, levels, group, groups, table, raw_hbm, flow_hbm, lev_hbm, out_ref,
     raw, raw_flow, lev_ref, raw_lo, raw_hi, start, first, partial, lo, hi, relay, pack_up, pack_dn, pack_lo, pack_hi,
     flow, v_lo, v_hi, lev_lo, lev_hi, coef, edge, wets, halo,
     load, aux_load, send_up, send_dn, recv_lo, recv_hi, relay_in, relay_out,
@@ -109,13 +138,14 @@
     rest = nlon % LANES
     whole = nlon - rest
     chunks = planes // SUB
-    groups = [spans_of(x) for x in sizes]
-    cut = min(PACK_CUT, chunks - 1)
-    packs = [[(0, cut), (cut, chunks - cut)], [(0, chunks - cut), (chunks - cut, cut)]]
+    loads = spans_of(load_sizes(chunks))
+    offset = [0, len(groups[0])]
+    packs = [spans_of(x) for x in pack_sizes(chunks)]
+    first_pack = [0, len(packs[0])]
     layers = lat // group
     layer = me // group
     place = me % group
-    relays = layers > 1 and group > 2 and lat % group == 0
+    relays = bool(table)
     has_lo = me > 0
     has_hi = me < lat - 1
     is_first = place == 0
@@ -135,7 +165,7 @@
         return pl.ds(pl.multiple_of(g * SUB, SUB), SUB)
 
     def loading(i):
-        at, n = groups[0][i]
+        at, n = loads[i]
         part = pl.ds(at * SUB, n * SUB)
         return pltpu.make_async_copy(raw_hbm.at[part], raw.at[part], load.at[i])
 
@@ -150,7 +180,7 @@
     loading(0).start()
     flow_load.start()
 
-    for i in range(1, len(groups[0])):
+    for i in range(1, len(loads)):
         loading(i).start()
 
     def remote(src, dst, s, r, by):
@@ -173,43 +203,41 @@
     def unmasked(up):
         n = groups[0][0][1] * SUB
         src = raw_hbm.at[pl.ds(0, n), pl.ds(rows - HALO if up else 0, HALO), pl.ds(0, whole)]
-        s, r = (send_raw.at[0], recv_lo.at[0, 0]) if up else (send_raw.at[1], recv_hi.at[0, 0])
+        s, r = (send_raw.at[0], recv_lo.at[0]) if up else (send_raw.at[1], recv_hi.at[0])
         return remote(src, raw_lo if up else raw_hi, s, r, 1 if up else -1)
 
     def main(phase, up, i, via=False):
         skip = 0 if phase else groups[0][0][1]
-        at, n = (skip, chunks - skip) if i is None else groups[phase][i]
+        at, n, k, count = (skip, chunks - skip, 0, HALO) if i is None else groups[phase][i]
         part = pl.ds(at * SUB, n * SUB)
         own = first if phase else start
-        src = own.at[pl.ds(rows - HALO if up else 0, HALO), part, pl.ds(0, whole)]
+        src = own.at[pl.ds(k + (rows - HALO if up else 0), count), part, pl.ds(0, whole)]
         s = (send_up if up else send_dn).at[phase]
-        i = i or 0
+        r = offset[phase] + (i or 0)
         if via:
             by = 1 - group if up else group - 1
-            return remote(src, relay.at[phase, :, part], s, relay_in.at[phase, i], by)
-        dst = (lo if up else hi).at[phase, :, part]
-        r = (recv_lo if up else recv_hi).at[phase, i]
-        return remote(src, dst, s, r, 1 if up else -1)
+            return remote(src, relay.at[phase, pl.ds(k, count), part], s, relay_in.at[r], by)
+        dst = (lo if up else hi).at[phase, pl.ds(k, count), part]
+        return remote(src, dst, s, (recv_lo if up else recv_hi).at[r], 1 if up else -1)
 
     def ends_copy(phase, up, i):
         at, n = (0, chunks) if i is None else packs[phase][i]
         part = pl.ds(at, n)
-        i = i or 0
+        i = first_pack[phase] + (i or 0)
         if up:
             return remote(pack_up.at[phase, part], pack_lo.at[phase, part],
-                          psend_up.at[phase], precv_lo.at[phase, i], 1)
+                          psend_up.at[phase], precv_lo.at[i], 1)
         return remote(pack_dn.at[phase, part], pack_hi.at[phase, part],
-                      psend_dn.at[phase], precv_hi.at[phase, i], -1)
+                      psend_dn.at[phase], precv_hi.at[i], -1)
 
     def forward(phase, up, i):
-        at, n = groups[phase][i]
+        at, n, k, count = groups[phase][i]
         part = pl.ds(at * SUB, n * SUB)
-        dst = (lo if up else hi).at[phase, :, part]
-        r = (recv_lo if up else recv_hi).at[phase, i]
-        return remote(relay.at[phase, :, part], dst, relay_out.at[phase], r,
+        piece = pl.ds(k, count)
+        dst = (lo if up else hi).at[phase, piece, part]
+        r = (recv_lo if up else recv_hi).at[offset[phase] + i]
+        return remote(relay.at[phase, piece, part], dst, relay_out.at[phase], r,
                       group if up else -group)
-
-    table = detours(sizes, layers) if relays else []
 
     def bent(phase, i, share):
         result = False
@@ -218,8 +246,9 @@
                 result = result | (share == value)
         return result
 
-    bent_up = {(p, i): bent(p, i, layers - 1 - layer) for p in range(2) for i in range(len(sizes[p]))}
-    bent_dn = {(p, i): bent(p, i, layer) for p in range(2) for i in range(len(sizes[p]))}
+    names = [(p, i) for p in range(2) for i in range(len(groups[p]))]
+    bent_up = {name: bent(*name, layers - 1 - layer) for name in names}
+    bent_dn = {name: bent(*name, layer) for name in names}
     ways = ((True, has_hi, is_last, bent_up), (False, has_lo, is_first, bent_dn))
     duties = ((True, is_first, bent_up), (False, is_last, bent_dn))
 
@@ -273,14 +302,14 @@
                 copy(phase, up, i).wait_recv()
 
     def receive(phase, g):
-        for i, (at, _) in enumerate(groups[phase]):
+        for i, (at, _, _, _) in enumerate(groups[phase]):
             @pl.when(g == at)
             def _(i=i):
                 if i == 0:
-                    for j in range(min(LEAD, len(groups[phase]))):
+                    for j in range(min(LEAD[phase], len(groups[phase]))):
                         pass_on(phase, j)
-                if i + LEAD < len(groups[phase]):
-                    pass_on(phase, i + LEAD)
+                if i + LEAD[phase] < len(groups[phase]):
+                    pass_on(phase, i + LEAD[phase])
                 arrived(main if phase or i else lambda phase, up, i: unmasked(up), phase, i)
 
         for i, (at, _) in enumerate(packs[phase]):
@@ -289,7 +318,7 @@
                 arrived(ends_copy, phase, i)
 
     def dispatch(phase, g):
-        for i, (at, n) in enumerate(groups[phase]):
+        for i, (at, n, _, _) in enumerate(groups[phase]):
             if phase or i:
                 @pl.when(g == at + n - 1)
                 def _(i=i):
@@ -340,7 +369,7 @@
             flow[which, k] = raw_flow[which, :, k, :]
 
     def begin(g, carry):
-        for i, (at, _) in enumerate(groups[0]):
+        for i, (at, _) in enumerate(loads):
             if i:
                 @pl.when(g == at)
                 def _(i=i):
@@ -542,14 +571,19 @@
 
 
 def shards(group, tracers, currents, column_levels):
-    count, levels, rows, nlon = tracers.shape
-    planes = count * levels
+    tracer, levels, rows, nlon = tracers.shape
+    planes = tracer * levels
     width = -(-(nlon + 2 * WRAP) // LANES) * LANES
     whole = nlon - nlon % LANES
     raw = tracers.reshape(planes, rows, nlon)
     chunks = planes // SUB
-    sizes = [growing(chunks, AHEAD), growing(chunks, 1)[::-1]]
-    count = max(map(len, sizes))
+    groups = pieces_of(chunks)
+    count = len(groups[0]) + len(groups[1])
+    ends = sum(map(len, pack_sizes(chunks)))
+    lat = lax.axis_size("lat")
+    layers = lat // group
+    relays = layers > 1 and group > 2 and lat % group == 0
+    table = detours(groups, layers) if relays else []
     hbm = pl.BlockSpec(memory_space=pltpu.HBM)
     vmem = pl.BlockSpec(memory_space=pltpu.VMEM)
     dma = pltpu.SemaphoreType.DMA
@@ -563,7 +597,7 @@
     pack = f32(2, chunks, SUB // 2, LANES)
     args = [pltpu.with_memory_space_constraint(x, pltpu.HBM) for x in (raw, currents, column_levels)]
     out = pl.pallas_call(
-        functools.partial(kernel, nlon, levels, group, sizes),
+        functools.partial(kernel, nlon, levels, group, groups, table),
         out_shape=jax.ShapeDtypeStruct((planes, rows, nlon), jnp.float32),
         in_specs=[hbm] * 3,
         out_specs=vmem,
@@ -571,8 +605,8 @@
             f32(planes, rows, nlon),
             f32(*currents.shape),
             i32(*column_levels.shape),
-            f32(sizes[0][0] * SUB, HALO, whole),
-            f32(sizes[0][0] * SUB, HALO, whole),
+            f32(groups[0][0][1] * SUB, HALO, whole),
+            f32(groups[0][0][1] * SUB, HALO, whole),
             f32(rows, planes, width),
             f32(rows, planes, width),
             f32(rows, planes, width),
@@ -588,9 +622,9 @@
             f32(6, SUB, width),
             f32(rows + 2, SUB, width),
             f32(2 * HALO, SUB, width),
-            dma((len(sizes[0]),)), dma((2,)), dma((2,)), dma((2,)),
-            dma((2, count)), dma((2, count)), dma((2, count)), dma((2,)),
-            dma((2,)), dma((2,)), dma((2, 2)), dma((2, 2)), dma((4,)), dma((4,)), dma((2,)),
+            dma((len(load_sizes(chunks)),)), dma((2,)), dma((2,)), dma((2,)),
+            dma((count,)), dma((count,)), dma((count,)), dma((2,)),
+            dma((2,)), dma((2,)), dma((ends,)), dma((ends,)), dma((4,)), dma((4,)), dma((2,)),
         ],
         compiler_params=pltpu.CompilerParams(
             collective_id=0, has_side_effects=True, vmem_limit_bytes=44 * 1024 * 1024

time: 59.7 us -> 59.2 us (level); the launches traced: 58.6 us -> 59 us
  no operation moved by 1% of the time
where the time goes in v4:
time: 59.2 us; the launch traced here: 59 us
  Pallas kernels  57.4 us (97%)
  local copies, waits for them, and re-layouts  1.6 us (3%)
    pallas_call x1, Pallas kernels, shards(): pl.pallas_call(functools.partial(kernel, nlon, levels, group, groups, tab...  57.4 us
    unnamed x1, local copies, waits for them, and re-layouts  1.6 us

profile of v4, /device:TPU:9, one launch (start us, length us, event | category | flops | bytes accessed | tf_op | source)
XLA Modules:
  0.0 59.0 jit_solution(40783242674063405)
XLA Ops:
  0.0 57.4 %shard_map.37 = f32[120,4,1440]{2,1,0:T(4,128)S(1)} custom-call(f32[120,4,1440]{2,1,0:T(4,128)} %bitcast.3, f32[2,4,4,1440]{3,2,1,0:T(4,128)} %flow_hbm.1, s32[4,1440]{1,0:T(4,128)} %lev_hbm.1), custom_call_target="tpu_custom_call" | custom-call | tf_op jit(solution)/shard_map/pallas_call | solution.py:599
  57.4 1.6 %copy.5 = f32[30,4,4,1440]{3,2,1,0:T(4,128)} copy(f32[30,4,4,1440]{3,2,1,0:T(4,128)S(1)} %bitcast.2) | data formatting | bytes 5529600

commit v5 on v4

--- a/solution.py
+++ b/solution.py
@@ -90,7 +90,7 @@
     early = [PACK_CUT]
     while sum(early) < chunks:
         early.append(min(PACK_CUT + 1, chunks - sum(early)))
-    return [early, early[::-1]]
+    return [early, [chunks - PACK_CUT, PACK_CUT]]
 
 
 def pieces_of(chunks):
@@ -384,7 +384,6 @@
         return carry
 
     lax.fori_loop(1, chunks, begin, 0)
-    dispatch(0, chunks - 1)
 
     spans = [(q * LANES, min(LANES, nlon - q * LANES)) for q in range(width // LANES)]
 
@@ -452,6 +451,8 @@
 
     def north_face(j):
         return face_terms(0.5 * (v_row(j) + v_row(j + 1)), wets[j + 1] * wets[j + 2])
+
+    dispatch(0, chunks - 1)
 
     below = north_face(-1)
     for k in range(rows):

time: 59.2 us -> 59.1 us (level)
  no operation moved by 1% of the time
where the time goes in v5:
time: 59.1 us; the launch traced here: 59 us
  Pallas kernels  57.4 us (97%)
  local copies, waits for them, and re-layouts  1.6 us (3%)
    pallas_call x1, Pallas kernels, shards(): pl.pallas_call(functools.partial(kernel, nlon, levels, group, groups, tab...  57.4 us
    unnamed x1, local copies, waits for them, and re-layouts  1.6 us

profile of v5, /device:TPU:9, one launch (start us, length us, event | category | flops | bytes accessed | tf_op | source)
XLA Modules:
  0.0 59.0 jit_solution(9751065451422015505)
XLA Ops:
  0.0 57.4 %shard_map.37 = f32[120,4,1440]{2,1,0:T(4,128)S(1)} custom-call(f32[120,4,1440]{2,1,0:T(4,128)} %bitcast.3, f32[2,4,4,1440]{3,2,1,0:T(4,128)} %flow_hbm.1, s32[4,1440]{1,0:T(4,128)} %lev_hbm.1), custom_call_target="tpu_custom_call" | custom-call | tf_op jit(solution)/shard_map/pallas_call | solution.py:600
  57.4 1.6 %copy.5 = f32[30,4,4,1440]{3,2,1,0:T(4,128)} copy(f32[30,4,4,1440]{3,2,1,0:T(4,128)S(1)} %bitcast.2) | data formatting | bytes 5529600
